TPU v7x, 32 devices: a whole 2x2x4 slice. The times are simulated.
32 devices in a mesh: seq: 8 (over z, core), feat: 4 (over y, x).
Axes of the slice: x: 2, y: 2, z: 4, core: 2. Of those that a mesh axis runs over, the one named last changes fastest.
Arguments:
- activations: bfloat16 [2048, 6144], P('seq', 'feat'), may hold values from -15 to 15
- ridge_scale: float32 [], replicated, may hold values from 0.5 to 2
Outputs:
- whitened: bfloat16 [2048, 6144], P('seq', 'feat')
All inputs are finite; a program needn't handle non-finite values.
Results may differ from a plain program's by a relative error of at most 0.0033.
Values sent between devices are 32-bit elements; how exact they have to be, the bound alone decides.
A program may use at most 128 MiB of HBM per device.

v0:
```python
import jax
import jax.numpy as jnp
from jax import lax
from jax.sharding import PartitionSpec as P

RANK = 128
ROOT_STEPS = 12
precise = lax.Precision.HIGHEST


def partner_2(block, axis, bit):
    count = lax.axis_size(axis)
    route = []
    for low in range(count):
        high = low | 1 << bit
        if high != low and high < count:
            route += [(low, high), (high, low)]
    return lax.ppermute(block, axis, route)


def product(left_matrix, right_matrix):
    return jnp.dot(left_matrix, right_matrix, precision=precise)


def reduce_gram(stacked_gram):
    rank_size = stacked_gram.shape[0] // 2
    identity = jnp.eye(rank_size, dtype=stacked_gram.dtype)
    subspace = jnp.concatenate([identity, identity], axis=0) * 0.7071067811865476
    image_cols = product(stacked_gram, subspace)
    factor = jnp.linalg.cholesky(product(image_cols.T, image_cols))
    subspace = jax.scipy.linalg.solve_triangular(factor, image_cols.T, lower=True).T
    quotient = product(subspace.T, product(stacked_gram, subspace))
    quotient = 0.5 * (quotient + quotient.T)
    tail_mass = (jnp.trace(stacked_gram) - jnp.trace(quotient)) / rank_size
    root_factor = jnp.linalg.cholesky(quotient)
    inner_gram = product(root_factor.T, root_factor) + tail_mass * identity
    lower_factor = jnp.linalg.cholesky(inner_gram)
    return jax.scipy.linalg.solve_triangular(
        lower_factor, product(root_factor.T, subspace.T), lower=True
    )


def combine(earlier, later):
    own_gram, cross_gram, last_gram = lax.psum(
        (product(earlier, earlier.T), product(earlier, later.T), product(later, later.T)), "feat"
    )
    stacked_gram = jnp.concatenate(
        [jnp.concatenate([own_gram, cross_gram], 1), jnp.concatenate([cross_gram.T, last_gram], 1)],
        0,
    )
    mixing = reduce_gram(stacked_gram)
    return product(mixing, jnp.concatenate([earlier, later], 0))


def square_root(matrix):
    identity = jnp.eye(matrix.shape[0], dtype=matrix.dtype)
    norm_size = jnp.sqrt(jnp.sum(matrix * matrix))
    current = matrix / norm_size
    partner = identity
    for repeat in range(ROOT_STEPS):
        middle = 1.5 * identity - 0.5 * product(partner, current)
        current = product(current, middle)
        partner = product(middle, partner)
    return current * jnp.sqrt(norm_size)


def on_device(activations, ridge_scale):
    width = activations.shape[1]
    block_count = activations.shape[0] // (2 * RANK)
    block_rows = activations.reshape(block_count, 2 * RANK, width)
    partial_grams = jnp.einsum(
        "bik,bjk->bij", block_rows, block_rows, preferred_element_type=jnp.float32
    )
    slab_grams = lax.psum(partial_grams, "feat")
    mixtures = jax.vmap(reduce_gram)(slab_grams)
    sketches = jnp.einsum(
        "bij,bjk->bik", mixtures, block_rows.astype(jnp.float32), precision=precise
    )
    slab_sketch = sketches[0]
    levels = lax.axis_size("seq").bit_length() - 1
    seq_index = lax.axis_index("seq")
    tree_block = slab_sketch
    prefix = slab_sketch
    for tree_level in range(levels):
        partner = partner_2(tree_block, "seq", tree_level)
        merged = combine(partner, prefix)
        has_bit = seq_index // (1 << tree_level) % 2 == 1
        prefix = jnp.where(has_bit, merged, prefix)
        if tree_level + 1 < levels:
            tree_block = combine(tree_block, partner)
    seen_rows = ((seq_index + 1) * activations.shape[0]).astype(jnp.float32)
    scaled = prefix * lax.rsqrt(seen_rows * ridge_scale)
    half_basis = scaled.astype(jnp.bfloat16)
    small_gram, projection = lax.psum(
        (
            product(scaled, scaled.T),
            jnp.dot(activations, half_basis.T, preferred_element_type=jnp.float32),
        ),
        "feat",
    )
    identity = jnp.eye(small_gram.shape[0], dtype=small_gram.dtype)
    shifted = identity + small_gram
    total_gram = shifted + square_root(shifted)
    total_gram = 0.5 * (total_gram + total_gram.T)
    coefficients = jax.scipy.linalg.cho_solve(
        (jnp.linalg.cholesky(total_gram), True), projection.T
    ).T
    restored = jnp.dot(
        coefficients.astype(jnp.bfloat16), half_basis, preferred_element_type=jnp.float32
    )
    return ((activations.astype(jnp.float32) - restored) * lax.rsqrt(ridge_scale)).astype(
        jnp.bfloat16
    )


def solution(mesh):
    placed = (P("seq", "feat"), P())
    return jax.shard_map(
        on_device, mesh=mesh, in_specs=placed, out_specs=P("seq", "feat"), check_vma=False
    )
```

profile of v0, /device:TPU:0, one launch (start us, length us, event | category | flops | bytes accessed | tf_op | source)
XLA Modules:
  0.0 740.0 jit_solution(10634055439625661038)
XLA Ops:
  6.5 2.5 convolution_bitcast_fusion
  9.2 46.9 %all-reduce.10.cloned.1.call-done = f32[1,256,256]{2,1,0:T(8,128)} async-done(((f32[1,256,256]{2,1,0:T(8,128)}), f32[1,256,256]{2,1,0:T(8,128)}) %all-reduce.10.cloned.1.call-update) | async-done | bytes 262160 | tf_op jit(solution)/shard_map/psum | solution.py:74
  58.0 11.7 %custom-call.29 = f32[1,128,128]{2,1,0:T(8,128)S(1)} custom-call(f32[1,128,128]{2,1,0:T(8,128)S(1)} %fusion.75), custom_call_target="Cholesky" | custom-call | tf_op jit(solution)/shard_map/vmap(jit(cholesky))/cholesky | solution.py:30
  71.0 9.8 %custom-call.30 = f32[1,1,128,128]{2,3,1,0:T(8,128)S(1)} custom-call(f32[1,1,128,128]{3,2,1,0:T(8,128)S(1)} %fusion.60), custom_call_target="InvertDiagBlocksLowerTriangular" | custom-call | tf_op jit(solution)/shard_map/vmap(jit(_solve_triangular))/triangular_solve | solution.py:31
  82.7 11.7 %custom-call.31 = f32[1,128,128]{2,1,0:T(8,128)S(1)} custom-call(f32[1,128,128]{2,1,0:T(8,128)S(1)} %fusion.121), custom_call_target="Cholesky" | custom-call | tf_op jit(solution)/shard_map/vmap(jit(cholesky))/cholesky | solution.py:35
  99.3 11.7 %custom-call.32 = f32[1,128,128]{2,1,0:T(8,128)S(1)} custom-call(f32[1,128,128]{2,1,0:T(8,128)S(1)} %fusion.73), custom_call_target="Cholesky" | custom-call | tf_op jit(solution)/shard_map/vmap(jit(cholesky))/cholesky | solution.py:37
  112.4 9.8 %custom-call.33 = f32[1,1,128,128]{2,3,1,0:T(8,128)S(1)} custom-call(f32[1,1,128,128]{3,2,1,0:T(8,128)S(1)} %fusion.61), custom_call_target="InvertDiagBlocksLowerTriangular" | custom-call | tf_op jit(solution)/shard_map/vmap(jit(_solve_triangular))/triangular_solve | solution.py:38
  123.1 1.4 fusion.285
  125.3 1.4 fusion.296
  126.8 1.4 fusion.287
  129.9 43.2 %all-reduce.18.cloned.1.call-done = (f32[128,128]{1,0:T(8,128)}, f32[128,128]{1,0:T(8,128)}, f32[128,128]{1,0:T(8,128)}, f32[128,128]{0,1:T(8,128)}) async-done(((f32[128,128]{1,0:T(8,128)}, f32[128,128]{1,0:T(8,128)}, f32[128,128]{1,0:T(8,128)}, f32[128,128]{0,1:T(8,128)}), (f32[128,128]{1,0:T(8,128)}, f32[128,128]{1,0:T(8,128)}, f32[128,128]{1,0:T(8,128)}, ...) | async-done | bytes 262160 | tf_op jit(solution)/shard_map/psum | solution.py:44
  178.1 11.7 %cholesky.404 = f32[128,128]{1,0:T(8,128)S(1)} custom-call(f32[128,128]{1,0:T(8,128)S(1)} %fusion.101), custom_call_target="Cholesky" | custom-call | tf_op jit(solution)/shard_map/jit(cholesky)/cholesky | solution.py:30
  191.1 9.8 %custom-call.38 = f32[1,128,128]{1,2,0:T(8,128)S(1)} custom-call(f32[1,128,128]{2,1,0:T(8,128)S(1)} %fusion.66), custom_call_target="InvertDiagBlocksLowerTriangular" | custom-call | tf_op jit(solution)/shard_map/jit(_solve_triangular)/triangular_solve/custom-call.3 | solution.py:31
  202.7 12.1 %cholesky.415 = f32[128,128]{1,0:T(8,128)S(1)} custom-call(f32[128,128]{1,0:T(8,128)S(1)} %fusion.98), custom_call_target="Cholesky" | custom-call | tf_op jit(solution)/shard_map/jit(cholesky)/cholesky | solution.py:35
  218.7 11.7 %cholesky.426 = f32[128,128]{1,0:T(8,128)S(1)} custom-call(f32[128,128]{1,0:T(8,128)S(1)} %fusion.97), custom_call_target="Cholesky" | custom-call | tf_op jit(solution)/shard_map/jit(cholesky)/cholesky | solution.py:37
  231.8 9.8 %custom-call.39 = f32[1,128,128]{1,2,0:T(8,128)S(1)} custom-call(f32[1,128,128]{2,1,0:T(8,128)S(1)} %fusion.67), custom_call_target="InvertDiagBlocksLowerTriangular" | custom-call | tf_op jit(solution)/shard_map/jit(_solve_triangular)/triangular_solve/custom-call.3 | solution.py:38
  242.1 11.7 %cholesky.338 = f32[128,128]{1,0:T(8,128)S(1)} custom-call(f32[128,128]{1,0:T(8,128)S(1)} %fusion.115), custom_call_target="Cholesky" | custom-call | tf_op jit(solution)/shard_map/jit(cholesky)/cholesky | solution.py:30
  255.2 10.0 %custom-call.34 = f32[1,128,128]{1,2,0:T(8,128)S(1)} custom-call(f32[1,128,128]{2,1,0:T(8,128)S(1)} %fusion.62), custom_call_target="InvertDiagBlocksLowerTriangular" | custom-call | tf_op jit(solution)/shard_map/jit(_solve_triangular)/triangular_solve/custom-call.3 | solution.py:31
  267.0 11.7 %cholesky.349 = f32[128,128]{1,0:T(8,128)S(1)} custom-call(f32[128,128]{1,0:T(8,128)S(1)} %fusion.112), custom_call_target="Cholesky" | custom-call | tf_op jit(solution)/shard_map/jit(cholesky)/cholesky | solution.py:35
  282.5 11.7 %cholesky.360 = f32[128,128]{1,0:T(8,128)S(1)} custom-call(f32[128,128]{1,0:T(8,128)S(1)} %fusion.111), custom_call_target="Cholesky" | custom-call | tf_op jit(solution)/shard_map/jit(cholesky)/cholesky | solution.py:37
  295.6 10.2 %custom-call.35 = f32[1,128,128]{1,2,0:T(8,128)S(1)} custom-call(f32[1,128,128]{2,1,0:T(8,128)S(1)} %fusion.63), custom_call_target="InvertDiagBlocksLowerTriangular" | custom-call | tf_op jit(solution)/shard_map/jit(_solve_triangular)/triangular_solve/custom-call.3 | solution.py:38
  307.1 1.6 collective-permute-start.1
  312.8 13.1 %collective-permute-done.1 = f32[128,1536]{1,0:T(8,128)S(1)} collective-permute-done((f32[128,1536]{1,0:T(8,128)S(1)}, f32[128,1536]{1,0:T(8,128)S(1)}, u32[]{:S(2)}, u32[]{:S(2)}) %collective-permute-start.1) | collective-permute-done | bytes 786464 | tf_op jit(solution)/shard_map/ppermute | solution.py:18
  330.4 44.5 %all-reduce.16.cloned.1.call-done = (f32[128,128]{1,0:T(8,128)}, f32[128,128]{0,1:T(8,128)}, f32[128,128]{0,1:T(8,128)}, f32[128,128]{0,1:T(8,128)}, f32[128,128]{0,1:T(8,128)}) async-done(((f32[128,128]{1,0:T(8,128)}, f32[128,128]{0,1:T(8,128)}, f32[128,128]{0,1:T(8,128)}, f32[128,128]{0,1:T(8,128)}, f32[128,128]{0,1:T(8,128)}), (f32[128,128]{1,0:T(8,128)}, f32[128,128]{0,1:T(8,128)}, ...) | async-done | bytes 327696 | tf_op jit(solution)/shard_map/psum | solution.py:44
  378.5 11.7 %cholesky.437 = f32[128,128]{1,0:T(8,128)S(1)} custom-call(f32[128,128]{1,0:T(8,128)S(1)} %fusion.94), custom_call_target="Cholesky" | custom-call | tf_op jit(solution)/shard_map/jit(cholesky)/cholesky | solution.py:30
  391.5 9.8 %custom-call.40 = f32[1,128,128]{1,2,0:T(8,128)S(1)} custom-call(f32[1,128,128]{2,1,0:T(8,128)S(1)} %fusion.68), custom_call_target="InvertDiagBlocksLowerTriangular" | custom-call | tf_op jit(solution)/shard_map/jit(_solve_triangular)/triangular_solve/custom-call.3 | solution.py:31
  403.2 11.7 %cholesky.448 = f32[128,128]{1,0:T(8,128)S(1)} custom-call(f32[128,128]{1,0:T(8,128)S(1)} %fusion.91), custom_call_target="Cholesky" | custom-call | tf_op jit(solution)/shard_map/jit(cholesky)/cholesky | solution.py:35
  418.9 11.7 %cholesky.459 = f32[128,128]{1,0:T(8,128)S(1)} custom-call(f32[128,128]{1,0:T(8,128)S(1)} %fusion.90), custom_call_target="Cholesky" | custom-call | tf_op jit(solution)/shard_map/jit(cholesky)/cholesky | solution.py:37
  432.5 11.7 %cholesky.371 = f32[128,128]{1,0:T(8,128)S(1)} custom-call(f32[128,128]{1,0:T(8,128)S(1)} %fusion.108), custom_call_target="Cholesky" | custom-call | tf_op jit(solution)/shard_map/jit(cholesky)/cholesky | solution.py:30
  445.7 9.8 %custom-call.36 = f32[1,128,128]{1,2,0:T(8,128)S(1)} custom-call(f32[1,128,128]{2,1,0:T(8,128)S(1)} %fusion.64), custom_call_target="InvertDiagBlocksLowerTriangular" | custom-call | tf_op jit(solution)/shard_map/jit(_solve_triangular)/triangular_solve/custom-call.3 | solution.py:31
  458.0 11.7 %cholesky.382 = f32[128,128]{1,0:T(8,128)S(1)} custom-call(f32[128,128]{1,0:T(8,128)S(1)} %fusion.105), custom_call_target="Cholesky" | custom-call | tf_op jit(solution)/shard_map/jit(cholesky)/cholesky | solution.py:35
  474.5 11.7 %cholesky.393 = f32[128,128]{1,0:T(8,128)S(1)} custom-call(f32[128,128]{1,0:T(8,128)S(1)} %fusion.104), custom_call_target="Cholesky" | custom-call | tf_op jit(solution)/shard_map/jit(cholesky)/cholesky | solution.py:37
  487.7 9.8 %custom-call.37 = f32[1,128,128]{1,2,0:T(8,128)S(1)} custom-call(f32[1,128,128]{2,1,0:T(8,128)S(1)} %fusion.65), custom_call_target="InvertDiagBlocksLowerTriangular" | custom-call | tf_op jit(solution)/shard_map/jit(_solve_triangular)/triangular_solve/custom-call.3 | solution.py:38
  497.8 1.9 fusion.7
  499.7 2.4 collective-permute-start.2
  502.8 9.9 %custom-call.41 = f32[1,128,128]{1,2,0:T(8,128)S(1)} custom-call(f32[1,128,128]{2,1,0:T(8,128)S(1)} %fusion.69), custom_call_target="InvertDiagBlocksLowerTriangular" | custom-call | tf_op jit(solution)/shard_map/jit(_solve_triangular)/triangular_solve/custom-call.3 | solution.py:38
  515.4 21.0 %collective-permute-done.2 = f32[128,1536]{1,0:T(8,128)S(1)} collective-permute-done((f32[128,1536]{1,0:T(8,128)}, f32[128,1536]{1,0:T(8,128)S(1)}, u32[]{:S(2)}, u32[]{:S(2)}) %collective-permute-start.2) | collective-permute-done | bytes 786464 | tf_op jit(solution)/shard_map/ppermute | solution.py:18
  537.8 1.4 fusion.295
  540.0 42.5 %all-reduce.14.cloned.1.call-done = (f32[128,128]{1,0:T(8,128)}, f32[128,128]{0,1:T(8,128)}, f32[128,128]{0,1:T(8,128)}) async-done(((f32[128,128]{1,0:T(8,128)}, f32[128,128]{0,1:T(8,128)}, f32[128,128]{0,1:T(8,128)}), (f32[128,128]{1,0:T(8,128)}, f32[128,128]{0,1:T(8,128)}, f32[128,128]{0,1:T(8,128)})) %all-reduce.14.cloned.1.call-update) | async-done | bytes 196624 | tf_op jit(solution)/shard_map/psum | solution.py:44
  586.1 11.7 %cholesky.470 = f32[128,128]{1,0:T(8,128)S(1)} custom-call(f32[128,128]{1,0:T(8,128)S(1)} %fusion.87), custom_call_target="Cholesky" | custom-call | tf_op jit(solution)/shard_map/jit(cholesky)/cholesky | solution.py:30
  599.0 9.8 %custom-call.42 = f32[1,128,128]{1,2,0:T(8,128)S(1)} custom-call(f32[1,128,128]{2,1,0:T(8,128)S(1)} %fusion.70), custom_call_target="InvertDiagBlocksLowerTriangular" | custom-call | tf_op jit(solution)/shard_map/jit(_solve_triangular)/triangular_solve/custom-call.3 | solution.py:31
  610.7 11.7 %cholesky.481 = f32[128,128]{1,0:T(8,128)S(1)} custom-call(f32[128,128]{1,0:T(8,128)S(1)} %fusion.84), custom_call_target="Cholesky" | custom-call | tf_op jit(solution)/shard_map/jit(cholesky)/cholesky | solution.py:35
  626.7 11.7 %cholesky.492 = f32[128,128]{1,0:T(8,128)S(1)} custom-call(f32[128,128]{1,0:T(8,128)S(1)} %fusion.83), custom_call_target="Cholesky" | custom-call | tf_op jit(solution)/shard_map/jit(cholesky)/cholesky | solution.py:37
  639.9 9.8 %custom-call.43 = f32[1,128,128]{1,2,0:T(8,128)S(1)} custom-call(f32[1,128,128]{2,1,0:T(8,128)S(1)} %fusion.71), custom_call_target="InvertDiagBlocksLowerTriangular" | custom-call | tf_op jit(solution)/shard_map/jit(_solve_triangular)/triangular_solve/custom-call.3 | solution.py:38
  653.8 42.6 %all-reduce.12.cloned.1.call-done = (f32[128,256]{1,0:T(8,128)}, f32[128,128]{0,1:T(8,128)}) async-done(((f32[128,256]{1,0:T(8,128)}, f32[128,128]{0,1:T(8,128)}), (f32[128,256]{1,0:T(8,128)}, f32[128,128]{0,1:T(8,128)})) %all-reduce.12.cloned.1.call-update) | async-done | bytes 196624 | tf_op jit(solution)/shard_map/psum | solution.py:94
  696.4 1.5 multiply_reduce_fusion
  708.5 11.7 %cholesky.503 = f32[128,128]{1,0:T(8,128)S(1)} custom-call(f32[128,128]{1,0:T(8,128)S(1)} %copy.70), custom_call_target="Cholesky" | custom-call | tf_op jit(solution)/shard_map/jit(cholesky)/cholesky | solution.py:106
  721.5 9.8 %custom-call.44 = f32[1,128,128]{1,2,0:T(8,128)S(1)} custom-call(f32[1,128,128]{2,1,0:T(8,128)S(1)} %fusion.72), custom_call_target="InvertDiagBlocksLowerTriangular" | custom-call | tf_op jit(solution)/shard_map/jit(_cho_solve)/triangular_solve/custom-call.3 | solution.py:105
  (276 shorter events, 95.7 us)
Async XLA Ops:
  6.5 49.5 %all-reduce.10.cloned.1.call-start = ((), (), s32[]{:S(2)}) async-start(), calls=%async_computation | async-start | bytes 524288 | tf_op jit(solution)/shard_map/psum | solution.py:74
  9.1 164.0 %all-reduce.18.cloned.1.call-start = ((), (), s32[]{:S(2)}) async-start(), calls=%async_computation.4 | async-start | bytes 524288 | tf_op jit(solution)/shard_map/psum | solution.py:44
  56.1 25.1 %copy-start.6 = (f32[1,256,256]{2,1,0:T(8,128)S(1)}, f32[1,256,256]{2,1,0:T(8,128)}, u32[]{:S(2)}) copy-start(f32[1,256,256]{2,1,0:T(8,128)} %all-reduce.10.cloned.1.call-done) | copy-start | bytes 786436
  95.1 27.4 %copy-start.2 = (bf16[256,1536]{1,0:T(8,128)(2,1)S(1)}, bf16[256,1536]{1,0:T(8,128)(2,1)}, u32[]{:S(2)}) copy-start(bf16[256,1536]{1,0:T(8,128)(2,1)} %param.8) | copy-start | bytes 2359300
  123.0 2.4 collective-permute-start
  129.6 245.3 %all-reduce.16.cloned.1.call-start = ((), (), s32[]{:S(2)}) async-start(), calls=%async_computation.3 | async-start | bytes 655360 | tf_op jit(solution)/shard_map/psum | solution.py:44
  173.1 2.9 copy-start.8
  173.1 2.9 copy-start.9
  173.1 2.9 copy-start.12
  173.1 3.3 copy-start.11
  307.1 21.6 %copy-start = (f32[128,1536]{1,0:T(8,128)}, f32[128,1536]{1,0:T(8,128)S(1)}, u32[]{:S(2)}) copy-start(f32[128,1536]{1,0:T(8,128)S(1)} %fusion.3) | copy-start | bytes 2359300
  307.1 18.8 %collective-permute-start.1 = (f32[128,1536]{1,0:T(8,128)S(1)}, f32[128,1536]{1,0:T(8,128)S(1)}, u32[]{:S(2)}, u32[]{:S(2)}) collective-permute-start(f32[128,1536]{1,0:T(8,128)S(1)} %fusion.3), channel_id=1, source_target_pairs={{0,8},{8,0},{4,12},{12,4},{16,24},{24,16},{20,28},{28,20},{1,9},{9... | collective-permute-start | bytes 2359304 | tf_op jit(solution)/shard_map/ppermute | solution.py:18
  330.2 252.4 %all-reduce.14.cloned.1.call-start = ((), (), s32[]{:S(2)}) async-start(), calls=%async_computation.2 | async-start | bytes 393216 | tf_op jit(solution)/shard_map/psum | solution.py:44
  374.9 2.3 copy-start.14
  374.9 2.3 copy-start.18
  402.3 29.0 %copy-start.7 = (f32[128,128]{0,1:T(8,128)S(1)}, f32[128,128]{0,1:T(8,128)}, u32[]{:S(2)}) copy-start(f32[128,128]{0,1:T(8,128)} %get-tuple-element.19) | copy-start | bytes 196612
  402.4 29.0 %copy-start.10 = (f32[128,128]{0,1:T(8,128)S(1)}, f32[128,128]{0,1:T(8,128)}, u32[]{:S(2)}) copy-start(f32[128,128]{0,1:T(8,128)} %get-tuple-element.18) | copy-start | bytes 196612
  402.4 29.0 %copy-start.16 = (f32[128,128]{0,1:T(8,128)S(1)}, f32[128,128]{0,1:T(8,128)}, u32[]{:S(2)}) copy-start(f32[128,128]{0,1:T(8,128)} %get-tuple-element.20) | copy-start | bytes 196612
  470.4 27.4 %copy-start.1 = (f32[128,1536]{1,0:T(8,128)S(1)}, f32[128,1536]{1,0:T(8,128)}, u32[]{:S(2)}) copy-start(f32[128,1536]{1,0:T(8,128)} %copy-done) | copy-start | bytes 2359300
  499.7 36.7 %collective-permute-start.2 = (f32[128,1536]{1,0:T(8,128)}, f32[128,1536]{1,0:T(8,128)S(1)}, u32[]{:S(2)}, u32[]{:S(2)}) collective-permute-start(f32[128,1536]{1,0:T(8,128)} %fusion.7), channel_id=1, source_target_pairs={{0,16},{16,0},{4,20},{20,4},{8,24},{24,8},{12,28},{28,12},{1,17},{... | collective-permute-start | bytes 2359304 | tf_op jit(solution)/shard_map/ppermute | solution.py:18
  536.4 1.4 copy-start.4
  539.3 157.2 %all-reduce.12.cloned.1.call-start = ((), (), s32[]{:S(2)}) async-start(), calls=%async_computation.1 | async-start | bytes 393216 | tf_op jit(solution)/shard_map/psum | solution.py:94
  582.5 2.3 copy-start.13
  582.5 2.3 copy-start.17
  610.6 39.4 %copy-start.5 = (f32[128,1536]{1,0:T(8,128)S(1)}, f32[128,1536]{1,0:T(8,128)}, u32[]{:S(2)}) copy-start(f32[128,1536]{1,0:T(8,128)} %copy-done.4) | copy-start | bytes 2359300
  650.0 1.1 copy-start.3
  705.9 1.9 copy-start.15
  707.2 24.2 %copy-start.19 = (f32[128,256]{1,0:T(8,128)S(1)}, f32[128,256]{1,0:T(8,128)}, u32[]{:S(2)}) copy-start(f32[128,256]{1,0:T(8,128)} %get-tuple-element.10) | copy-start | bytes 393220
Sparse Core Ops, SparseCore 0:
  10.3 45.7 all-reduce.9
  129.7 43.3 all-reduce.17
  330.3 44.6 all-reduce.15
  539.4 43.1 all-reduce.13
  653.8 42.6 all-reduce.11
where the time goes:
time: 750 us; the launch traced here: 740 us
  other arithmetic  385 us (51%)
  waiting for transfers between devices  255 us (34%)
  matrix products  66.9 us (9%)
  between operations  23.9 us (3%)
    psum x3, waiting for transfers between devices, combine(): lax.psum((product(earlier, earlier.T), product(earlier, later.T), product...  130 us
    another operation x18, other arithmetic, reduce_gram(): root_factor = jnp.linalg.cholesky(quotient)  74.9 us
    another operation x18, other arithmetic, reduce_gram(): lower_factor = jnp.linalg.cholesky(inner_gram)  74.6 us
    another operation x18, other arithmetic, reduce_gram(): factor = jnp.linalg.cholesky(product(image_cols.T, image_cols))  74.4 us
    another operation x12, other arithmetic, reduce_gram(): jax.scipy.linalg.solve_triangular(lower_factor, product(root_factor.T, su...  63.4 us
    another operation x12, other arithmetic, reduce_gram(): jax.scipy.linalg.solve_triangular(factor, image_cols.T, lower=True)  62.9 us
    dot_general x89, matrix products, product(): return jnp.dot(left_matrix, right_matrix, precision=precise)  57.2 us
    psum x1, waiting for transfers between devices, on_device(): slab_grams = lax.psum(partial_grams, 'feat')  46.9 us
  transfers between devices with their start and end apart: 8, of which 8 were waited for; matrix products, arithmetic and copies ran while one was open for 3% of the time, Pallas kernels for 0%

commit v1 on v0

--- a/solution.py
+++ b/solution.py
@@ -71,7 +71,8 @@
     partial_grams = jnp.einsum(
         "bik,bjk->bij", block_rows, block_rows, preferred_element_type=jnp.float32
     )
-    slab_grams = lax.psum(partial_grams, "feat")
+    shards = lax.all_gather(partial_grams, "feat")
+    slab_grams = jnp.sum(shards, axis=0)
     mixtures = jax.vmap(reduce_gram)(slab_grams)
     sketches = jnp.einsum(
         "bij,bjk->bik", mixtures, block_rows.astype(jnp.float32), precision=precise

time: 750 us -> 735 us (0.980)
  waiting for transfers between devices: 255 us -> 237 us
    psum x1 -> x0, waiting for transfers between devices: 46.9 us -> none  [on_device(): slab_grams = lax.psum(partial_grams, 'feat')]
    all_gather x0 -> x1, waiting for transfers between devices: none -> 29.3 us  [on_device(): shards = lax.all_gather(partial_grams, 'feat')]
where the time goes in v1:
time: 735 us; the launch traced here: 725 us
  other arithmetic  388 us (53%)
  waiting for transfers between devices  237 us (32%)
  matrix products  66.8 us (9%)
  between operations  24 us (3%)
    psum x3, waiting for transfers between devices, combine(): lax.psum((product(earlier, earlier.T), product(earlier, later.T), product...  130 us
    another operation x18, other arithmetic, reduce_gram(): root_factor = jnp.linalg.cholesky(quotient)  74.9 us
    another operation x18, other arithmetic, reduce_gram(): lower_factor = jnp.linalg.cholesky(inner_gram)  74.6 us
    another operation x18, other arithmetic, reduce_gram(): factor = jnp.linalg.cholesky(product(image_cols.T, image_cols))  74.5 us
    another operation x12, other arithmetic, reduce_gram(): jax.scipy.linalg.solve_triangular(lower_factor, product(root_factor.T, su...  63.4 us
    another operation x12, other arithmetic, reduce_gram(): jax.scipy.linalg.solve_triangular(factor, image_cols.T, lower=True)  62.9 us
    dot_general x89, matrix products, product(): return jnp.dot(left_matrix, right_matrix, precision=precise)  57.1 us
    psum x1, waiting for transfers between devices, on_device(): lax.psum((product(scaled, scaled.T), jnp.dot(activations, half_basis.T, p...  42.6 us
  transfers between devices with their start and end apart: 8, of which 8 were waited for; matrix products, arithmetic and copies ran while one was open for 3% of the time, Pallas kernels for 0%

profile of v1, /device:TPU:0, one launch (start us, length us, event | category | flops | bytes accessed | tf_op | source)
XLA Modules:
  0.0 725.3 jit_solution(8483613415419710054)
XLA Ops:
  6.5 2.5 fusion.279
  9.1 29.3 %all-gather.3.cloned.1.call-done = f32[1024,256]{1,0:T(8,128)} async-done(((f32[256,256]{1,0:T(8,128)}), f32[1024,256]{1,0:T(8,128)}) %all-gather.3.cloned.1.call-update) | async-done | bytes 1048592 | tf_op jit(solution)/shard_map/all_gather | solution.py:74
  41.3 11.7 %custom-call.29 = f32[1,128,128]{2,1,0:T(8,128)S(1)} custom-call(f32[1,128,128]{2,1,0:T(8,128)S(1)} %fusion.72), custom_call_target="Cholesky" | custom-call | tf_op jit(solution)/shard_map/vmap(jit(cholesky))/cholesky | solution.py:30
  54.3 9.8 %custom-call.30 = f32[1,1,128,128]{2,3,1,0:T(8,128)S(1)} custom-call(f32[1,1,128,128]{3,2,1,0:T(8,128)S(1)} %fusion.57), custom_call_target="InvertDiagBlocksLowerTriangular" | custom-call | tf_op jit(solution)/shard_map/vmap(jit(_solve_triangular))/triangular_solve | solution.py:31
  66.0 11.7 %custom-call.31 = f32[1,128,128]{2,1,0:T(8,128)S(1)} custom-call(f32[1,128,128]{2,1,0:T(8,128)S(1)} %fusion.118), custom_call_target="Cholesky" | custom-call | tf_op jit(solution)/shard_map/vmap(jit(cholesky))/cholesky | solution.py:35
  81.9 11.7 %custom-call.32 = f32[1,128,128]{2,1,0:T(8,128)S(1)} custom-call(f32[1,128,128]{2,1,0:T(8,128)S(1)} %fusion.70), custom_call_target="Cholesky" | custom-call | tf_op jit(solution)/shard_map/vmap(jit(cholesky))/cholesky | solution.py:37
  95.0 9.8 %custom-call.33 = f32[1,1,128,128]{2,3,1,0:T(8,128)S(1)} custom-call(f32[1,1,128,128]{3,2,1,0:T(8,128)S(1)} %fusion.58), custom_call_target="InvertDiagBlocksLowerTriangular" | custom-call | tf_op jit(solution)/shard_map/vmap(jit(_solve_triangular))/triangular_solve | solution.py:38
  105.7 1.4 fusion.284
  112.5 43.2 %all-reduce.15.cloned.1.call-done = (f32[128,128]{1,0:T(8,128)}, f32[128,128]{1,0:T(8,128)}, f32[128,128]{1,0:T(8,128)}, f32[128,128]{0,1:T(8,128)}) async-done(((f32[128,128]{1,0:T(8,128)}, f32[128,128]{1,0:T(8,128)}, f32[128,128]{1,0:T(8,128)}, f32[128,128]{0,1:T(8,128)}), (f32[128,128]{1,0:T(8,128)}, f32[128,128]{1,0:T(8,128)}, f32[128,128]{1,0:T(8,128)}, ...) | async-done | bytes 262160 | tf_op jit(solution)/shard_map/psum | solution.py:44
  161.5 11.7 %cholesky.404 = f32[128,128]{1,0:T(8,128)S(1)} custom-call(f32[128,128]{1,0:T(8,128)S(1)} %fusion.98), custom_call_target="Cholesky" | custom-call | tf_op jit(solution)/shard_map/jit(cholesky)/cholesky | solution.py:30
  174.6 9.8 %custom-call.38 = f32[1,128,128]{1,2,0:T(8,128)S(1)} custom-call(f32[1,128,128]{2,1,0:T(8,128)S(1)} %fusion.63), custom_call_target="InvertDiagBlocksLowerTriangular" | custom-call | tf_op jit(solution)/shard_map/jit(_solve_triangular)/triangular_solve/custom-call.3 | solution.py:31
  186.2 12.1 %cholesky.415 = f32[128,128]{1,0:T(8,128)S(1)} custom-call(f32[128,128]{1,0:T(8,128)S(1)} %fusion.95), custom_call_target="Cholesky" | custom-call | tf_op jit(solution)/shard_map/jit(cholesky)/cholesky | solution.py:35
  202.2 11.7 %cholesky.426 = f32[128,128]{1,0:T(8,128)S(1)} custom-call(f32[128,128]{1,0:T(8,128)S(1)} %fusion.94), custom_call_target="Cholesky" | custom-call | tf_op jit(solution)/shard_map/jit(cholesky)/cholesky | solution.py:37
  215.3 9.8 %custom-call.39 = f32[1,128,128]{1,2,0:T(8,128)S(1)} custom-call(f32[1,128,128]{2,1,0:T(8,128)S(1)} %fusion.64), custom_call_target="InvertDiagBlocksLowerTriangular" | custom-call | tf_op jit(solution)/shard_map/jit(_solve_triangular)/triangular_solve/custom-call.3 | solution.py:38
  225.6 11.7 %cholesky.338 = f32[128,128]{1,0:T(8,128)S(1)} custom-call(f32[128,128]{1,0:T(8,128)S(1)} %fusion.112), custom_call_target="Cholesky" | custom-call | tf_op jit(solution)/shard_map/jit(cholesky)/cholesky | solution.py:30
  238.6 9.9 %custom-call.34 = f32[1,128,128]{1,2,0:T(8,128)S(1)} custom-call(f32[1,128,128]{2,1,0:T(8,128)S(1)} %fusion.59), custom_call_target="InvertDiagBlocksLowerTriangular" | custom-call | tf_op jit(solution)/shard_map/jit(_solve_triangular)/triangular_solve/custom-call.3 | solution.py:31
  250.4 11.7 %cholesky.349 = f32[128,128]{1,0:T(8,128)S(1)} custom-call(f32[128,128]{1,0:T(8,128)S(1)} %fusion.109), custom_call_target="Cholesky" | custom-call | tf_op jit(solution)/shard_map/jit(cholesky)/cholesky | solution.py:35
  266.0 11.7 %cholesky.360 = f32[128,128]{1,0:T(8,128)S(1)} custom-call(f32[128,128]{1,0:T(8,128)S(1)} %fusion.108), custom_call_target="Cholesky" | custom-call | tf_op jit(solution)/shard_map/jit(cholesky)/cholesky | solution.py:37
  279.0 10.2 %custom-call.35 = f32[1,128,128]{1,2,0:T(8,128)S(1)} custom-call(f32[1,128,128]{2,1,0:T(8,128)S(1)} %fusion.60), custom_call_target="InvertDiagBlocksLowerTriangular" | custom-call | tf_op jit(solution)/shard_map/jit(_solve_triangular)/triangular_solve/custom-call.3 | solution.py:38
  290.5 1.6 collective-permute-start.1
  296.2 13.1 %collective-permute-done.1 = f32[128,1536]{1,0:T(8,128)S(1)} collective-permute-done((f32[128,1536]{1,0:T(8,128)S(1)}, f32[128,1536]{1,0:T(8,128)S(1)}, u32[]{:S(2)}, u32[]{:S(2)}) %collective-permute-start.1) | collective-permute-done | bytes 786464 | tf_op jit(solution)/shard_map/ppermute | solution.py:18
  313.9 44.5 %all-reduce.13.cloned.1.call-done = (f32[128,128]{1,0:T(8,128)}, f32[128,128]{0,1:T(8,128)}, f32[128,128]{0,1:T(8,128)}, f32[128,128]{0,1:T(8,128)}, f32[128,128]{0,1:T(8,128)}) async-done(((f32[128,128]{1,0:T(8,128)}, f32[128,128]{0,1:T(8,128)}, f32[128,128]{0,1:T(8,128)}, f32[128,128]{0,1:T(8,128)}, f32[128,128]{0,1:T(8,128)}), (f32[128,128]{1,0:T(8,128)}, f32[128,128]{0,1:T(8,128)}, ...) | async-done | bytes 327696 | tf_op jit(solution)/shard_map/psum | solution.py:44
  360.6 1.6 select_reduce_fusion.1
  362.7 11.7 %cholesky.437 = f32[128,128]{1,0:T(8,128)S(1)} custom-call(f32[128,128]{1,0:T(8,128)S(1)} %fusion.91), custom_call_target="Cholesky" | custom-call | tf_op jit(solution)/shard_map/jit(cholesky)/cholesky | solution.py:30
  375.7 9.8 %custom-call.40 = f32[1,128,128]{1,2,0:T(8,128)S(1)} custom-call(f32[1,128,128]{2,1,0:T(8,128)S(1)} %fusion.65), custom_call_target="InvertDiagBlocksLowerTriangular" | custom-call | tf_op jit(solution)/shard_map/jit(_solve_triangular)/triangular_solve/custom-call.3 | solution.py:31
  387.4 11.7 %cholesky.448 = f32[128,128]{1,0:T(8,128)S(1)} custom-call(f32[128,128]{1,0:T(8,128)S(1)} %fusion.88), custom_call_target="Cholesky" | custom-call | tf_op jit(solution)/shard_map/jit(cholesky)/cholesky | solution.py:35
  403.4 11.7 %cholesky.459 = f32[128,128]{1,0:T(8,128)S(1)} custom-call(f32[128,128]{1,0:T(8,128)S(1)} %fusion.87), custom_call_target="Cholesky" | custom-call | tf_op jit(solution)/shard_map/jit(cholesky)/cholesky | solution.py:37
  417.0 11.7 %cholesky.371 = f32[128,128]{1,0:T(8,128)S(1)} custom-call(f32[128,128]{1,0:T(8,128)S(1)} %fusion.105), custom_call_target="Cholesky" | custom-call | tf_op jit(solution)/shard_map/jit(cholesky)/cholesky | solution.py:30
  430.2 9.8 %custom-call.36 = f32[1,128,128]{1,2,0:T(8,128)S(1)} custom-call(f32[1,128,128]{2,1,0:T(8,128)S(1)} %fusion.61), custom_call_target="InvertDiagBlocksLowerTriangular" | custom-call | tf_op jit(solution)/shard_map/jit(_solve_triangular)/triangular_solve/custom-call.3 | solution.py:31
  442.5 11.7 %cholesky.382 = f32[128,128]{1,0:T(8,128)S(1)} custom-call(f32[128,128]{1,0:T(8,128)S(1)} %fusion.102), custom_call_target="Cholesky" | custom-call | tf_op jit(solution)/shard_map/jit(cholesky)/cholesky | solution.py:35
  458.9 11.7 %cholesky.393 = f32[128,128]{1,0:T(8,128)S(1)} custom-call(f32[128,128]{1,0:T(8,128)S(1)} %fusion.101), custom_call_target="Cholesky" | custom-call | tf_op jit(solution)/shard_map/jit(cholesky)/cholesky | solution.py:37
  472.1 9.8 %custom-call.37 = f32[1,128,128]{1,2,0:T(8,128)S(1)} custom-call(f32[1,128,128]{2,1,0:T(8,128)S(1)} %fusion.62), custom_call_target="InvertDiagBlocksLowerTriangular" | custom-call | tf_op jit(solution)/shard_map/jit(_solve_triangular)/triangular_solve/custom-call.3 | solution.py:38
  482.2 1.9 fusion.7
  484.1 2.4 collective-permute-start.2
  487.2 10.0 %custom-call.41 = f32[1,128,128]{1,2,0:T(8,128)S(1)} custom-call(f32[1,128,128]{2,1,0:T(8,128)S(1)} %fusion.66), custom_call_target="InvertDiagBlocksLowerTriangular" | custom-call | tf_op jit(solution)/shard_map/jit(_solve_triangular)/triangular_solve/custom-call.3 | solution.py:38
  499.8 21.0 %collective-permute-done.2 = f32[128,1536]{1,0:T(8,128)S(1)} collective-permute-done((f32[128,1536]{1,0:T(8,128)}, f32[128,1536]{1,0:T(8,128)S(1)}, u32[]{:S(2)}, u32[]{:S(2)}) %collective-permute-start.2) | collective-permute-done | bytes 786464 | tf_op jit(solution)/shard_map/ppermute | solution.py:18
  522.2 1.4 fusion.294
  524.4 42.5 %all-reduce.11.cloned.1.call-done = (f32[128,128]{1,0:T(8,128)}, f32[128,128]{0,1:T(8,128)}, f32[128,128]{0,1:T(8,128)}) async-done(((f32[128,128]{1,0:T(8,128)}, f32[128,128]{0,1:T(8,128)}, f32[128,128]{0,1:T(8,128)}), (f32[128,128]{1,0:T(8,128)}, f32[128,128]{0,1:T(8,128)}, f32[128,128]{0,1:T(8,128)})) %all-reduce.11.cloned.1.call-update) | async-done | bytes 196624 | tf_op jit(solution)/shard_map/psum | solution.py:44
  569.2 1.5 select_reduce_fusion
  571.2 11.7 %cholesky.470 = f32[128,128]{1,0:T(8,128)S(1)} custom-call(f32[128,128]{1,0:T(8,128)S(1)} %fusion.84), custom_call_target="Cholesky" | custom-call | tf_op jit(solution)/shard_map/jit(cholesky)/cholesky | solution.py:30
  584.4 9.8 %custom-call.42 = f32[1,128,128]{1,2,0:T(8,128)S(1)} custom-call(f32[1,128,128]{2,1,0:T(8,128)S(1)} %fusion.67), custom_call_target="InvertDiagBlocksLowerTriangular" | custom-call | tf_op jit(solution)/shard_map/jit(_solve_triangular)/triangular_solve/custom-call.3 | solution.py:31
  596.1 11.7 %cholesky.481 = f32[128,128]{1,0:T(8,128)S(1)} custom-call(f32[128,128]{1,0:T(8,128)S(1)} %fusion.81), custom_call_target="Cholesky" | custom-call | tf_op jit(solution)/shard_map/jit(cholesky)/cholesky | solution.py:35
  612.0 11.7 %cholesky.492 = f32[128,128]{1,0:T(8,128)S(1)} custom-call(f32[128,128]{1,0:T(8,128)S(1)} %fusion.80), custom_call_target="Cholesky" | custom-call | tf_op jit(solution)/shard_map/jit(cholesky)/cholesky | solution.py:37
  625.2 9.8 %custom-call.43 = f32[1,128,128]{1,2,0:T(8,128)S(1)} custom-call(f32[1,128,128]{2,1,0:T(8,128)S(1)} %fusion.68), custom_call_target="InvertDiagBlocksLowerTriangular" | custom-call | tf_op jit(solution)/shard_map/jit(_solve_triangular)/triangular_solve/custom-call.3 | solution.py:38
  639.1 42.6 %all-reduce.9.cloned.1.call-done = (f32[128,256]{1,0:T(8,128)}, f32[128,128]{0,1:T(8,128)}) async-done(((f32[128,256]{1,0:T(8,128)}, f32[128,128]{0,1:T(8,128)}), (f32[128,256]{1,0:T(8,128)}, f32[128,128]{0,1:T(8,128)})) %all-reduce.9.cloned.1.call-update) | async-done | bytes 196624 | tf_op jit(solution)/shard_map/psum | solution.py:95
  681.7 1.5 multiply_reduce_fusion
  693.8 11.7 %cholesky.503 = f32[128,128]{1,0:T(8,128)S(1)} custom-call(f32[128,128]{1,0:T(8,128)S(1)} %copy.70), custom_call_target="Cholesky" | custom-call | tf_op jit(solution)/shard_map/jit(cholesky)/cholesky | solution.py:107
  706.8 9.8 %custom-call.44 = f32[1,128,128]{1,2,0:T(8,128)S(1)} custom-call(f32[1,128,128]{2,1,0:T(8,128)S(1)} %fusion.69), custom_call_target="InvertDiagBlocksLowerTriangular" | custom-call | tf_op jit(solution)/shard_map/jit(_cho_solve)/triangular_solve/custom-call.3 | solution.py:106
  (275 shorter events, 98.3 us)
Async XLA Ops:
  6.5 31.9 %all-gather.3.cloned.1.call-start = ((), (), s32[]{:S(2)}) async-start(), calls=%async_computation | async-start | bytes 1310720 | tf_op jit(solution)/shard_map/all_gather | solution.py:74
  9.0 146.7 %all-reduce.15.cloned.1.call-start = ((), (), s32[]{:S(2)}) async-start(), calls=%async_computation.4 | async-start | bytes 524288 | tf_op jit(solution)/shard_map/psum | solution.py:44
  65.1 40.0 %copy-start.2 = (bf16[256,1536]{1,0:T(8,128)(2,1)S(1)}, bf16[256,1536]{1,0:T(8,128)(2,1)}, u32[]{:S(2)}) copy-start(bf16[256,1536]{1,0:T(8,128)(2,1)} %param.8) | copy-start | bytes 2359300
  105.6 2.4 collective-permute-start
  112.2 246.2 %all-reduce.13.cloned.1.call-start = ((), (), s32[]{:S(2)}) async-start(), calls=%async_computation.3 | async-start | bytes 655360 | tf_op jit(solution)/shard_map/psum | solution.py:44
  155.7 4.2 copy-start.7
  155.7 4.2 copy-start.8
  155.7 4.2 copy-start.10
  155.7 4.2 copy-start.11
  290.5 21.6 %copy-start = (f32[128,1536]{1,0:T(8,128)}, f32[128,1536]{1,0:T(8,128)S(1)}, u32[]{:S(2)}) copy-start(f32[128,1536]{1,0:T(8,128)S(1)} %fusion.3) | copy-start | bytes 2359300
  290.5 18.8 %collective-permute-start.1 = (f32[128,1536]{1,0:T(8,128)S(1)}, f32[128,1536]{1,0:T(8,128)S(1)}, u32[]{:S(2)}, u32[]{:S(2)}) collective-permute-start(f32[128,1536]{1,0:T(8,128)S(1)} %fusion.3), channel_id=1, source_target_pairs={{0,8},{8,0},{4,12},{12,4},{16,24},{24,16},{20,28},{28,20},{1,9},{9... | collective-permute-start | bytes 2359304 | tf_op jit(solution)/shard_map/ppermute | solution.py:18
  313.6 253.4 %all-reduce.11.cloned.1.call-start = ((), (), s32[]{:S(2)}) async-start(), calls=%async_computation.2 | async-start | bytes 393216 | tf_op jit(solution)/shard_map/psum | solution.py:44
  359.3 26.6 %copy-start.13 = (f32[128,128]{0,1:T(8,128)S(1)}, f32[128,128]{0,1:T(8,128)}, u32[]{:S(2)}) copy-start(f32[128,128]{0,1:T(8,128)} %get-tuple-element.17) | copy-start | bytes 196612
  359.3 26.6 %copy-start.17 = (f32[128,128]{1,0:T(8,128)S(1)}, f32[128,128]{1,0:T(8,128)}, u32[]{:S(2)}) copy-start(f32[128,128]{1,0:T(8,128)} %get-tuple-element.16) | copy-start | bytes 196612
  386.2 29.6 %copy-start.6 = (f32[128,128]{0,1:T(8,128)S(1)}, f32[128,128]{0,1:T(8,128)}, u32[]{:S(2)}) copy-start(f32[128,128]{0,1:T(8,128)} %get-tuple-element.19) | copy-start | bytes 196612
  386.3 29.7 %copy-start.9 = (f32[128,128]{0,1:T(8,128)S(1)}, f32[128,128]{0,1:T(8,128)}, u32[]{:S(2)}) copy-start(f32[128,128]{0,1:T(8,128)} %get-tuple-element.18) | copy-start | bytes 196612
  386.3 29.7 %copy-start.15 = (f32[128,128]{0,1:T(8,128)S(1)}, f32[128,128]{0,1:T(8,128)}, u32[]{:S(2)}) copy-start(f32[128,128]{0,1:T(8,128)} %get-tuple-element.20) | copy-start | bytes 196612
  442.3 39.9 %copy-start.1 = (f32[128,1536]{1,0:T(8,128)S(1)}, f32[128,1536]{1,0:T(8,128)}, u32[]{:S(2)}) copy-start(f32[128,1536]{1,0:T(8,128)} %copy-done) | copy-start | bytes 2359300
  484.1 36.7 %collective-permute-start.2 = (f32[128,1536]{1,0:T(8,128)}, f32[128,1536]{1,0:T(8,128)S(1)}, u32[]{:S(2)}, u32[]{:S(2)}) collective-permute-start(f32[128,1536]{1,0:T(8,128)} %fusion.7), channel_id=1, source_target_pairs={{0,16},{16,0},{4,20},{20,4},{8,24},{24,8},{12,28},{28,12},{1,17},{... | collective-permute-start | bytes 2359304 | tf_op jit(solution)/shard_map/ppermute | solution.py:18
  520.8 2.8 copy-start.4
  523.7 158.1 %all-reduce.9.cloned.1.call-start = ((), (), s32[]{:S(2)}) async-start(), calls=%async_computation.1 | async-start | bytes 393216 | tf_op jit(solution)/shard_map/psum | solution.py:95
  567.8 26.7 %copy-start.12 = (f32[128,128]{0,1:T(8,128)S(1)}, f32[128,128]{0,1:T(8,128)}, u32[]{:S(2)}) copy-start(f32[128,128]{0,1:T(8,128)} %get-tuple-element.14) | copy-start | bytes 196612
  567.9 26.7 %copy-start.16 = (f32[128,128]{1,0:T(8,128)S(1)}, f32[128,128]{1,0:T(8,128)}, u32[]{:S(2)}) copy-start(f32[128,128]{1,0:T(8,128)} %get-tuple-element.13) | copy-start | bytes 196612
  595.2 40.1 %copy-start.5 = (f32[128,1536]{1,0:T(8,128)S(1)}, f32[128,1536]{1,0:T(8,128)}, u32[]{:S(2)}) copy-start(f32[128,1536]{1,0:T(8,128)} %copy-done.4) | copy-start | bytes 2359300
  635.3 1.1 copy-start.3
  690.8 2.4 copy-start.14
  692.1 24.6 %copy-start.18 = (f32[128,256]{1,0:T(8,128)S(1)}, f32[128,256]{1,0:T(8,128)}, u32[]{:S(2)}) copy-start(f32[128,256]{1,0:T(8,128)} %get-tuple-element.10) | copy-start | bytes 393220
Sparse Core Ops, SparseCore 0:
  9.2 29.2 all-gather.2
  112.3 43.3 all-reduce.14
  313.7 44.6 all-reduce.12
  523.8 43.1 all-reduce.10
  639.1 42.6 all-reduce.8
